TPU v7x, 32 devices: a whole 2x2x4 slice. The times are simulated.
32 devices in a mesh: grp: 4 (over y, x), col: 8 (over z, core).
Axes of the slice: x: 2, y: 2, z: 4, core: 2. Of those that a mesh axis runs over, the one named last changes fastest.
Arguments:
- panels: bfloat16 [32, 4, 512, 512], P('col', None, 'grp'), may hold values from -1.296875 to 1.296875
- parent: float32 [32, 512, 512], P('col', 'grp'), may hold values from -6 to 6
- src_block: int32 [8, 40], P('col'), may hold values from 0 to 39, each once within a row
- dest_owner: int32 [320, 1], P('col'), may hold values from 0 to 7; in each aligned block of 40 rows (0 to 39, 40 to 79, ...) at most 7 rows name the same one
- target: int32 [320], P('col'), may hold values from 0 to 3
- counts: int32 [8], P('col'), may hold values from 20 to 40, as said below
Outputs:
- assembled: float32 [32, 512, 512], P('col', 'grp')
Inputs may be any that keep to these rules, and one draw needn't show every extreme that they name: `src_block`: each row of a column rank is a permutation of the 40 block pairs. `dest_owner`: among the 40 slots of one column rank at most 7 name the same owner. The live slots of a rank are its first counts[c]; some rank has all 40 live.
All inputs are finite; a program needn't handle non-finite values.
Results may differ from a plain program's by a relative error of at most 0.0026.
Values may be sent and summed in bfloat16 or wider, within the bound.
A program may use at most 128 MiB of HBM per device.

v0:
```python
import functools

import jax
import jax.numpy as jnp
import numpy as np
from jax import lax
from jax.experimental import pallas as pl
from jax.experimental.pallas import tpu as pltpu
from jax.sharding import PartitionSpec as P

MESH = pl.DeviceIdType.MESH


def place_slots(src_block, dest_owner, target, counts, peer_count, capacity):
    slot_count = src_block.shape[1]
    slot_index = jnp.arange(slot_count, dtype=jnp.int32)
    owner_rank = dest_owner[:, 0]
    matches = (owner_rank[:, None] == jnp.arange(peer_count, dtype=jnp.int32)[None, :]).astype(
        jnp.int32
    )
    earlier = jnp.cumsum(matches, axis=0) - matches
    rank_in = jnp.sum(earlier * matches, axis=1)
    position = owner_rank * capacity + rank_in
    is_live = slot_index < counts[0]
    routed = jnp.zeros((peer_count * capacity,), jnp.int32).at[position].set(target)
    return (src_block[0], position, is_live, routed.reshape(peer_count, capacity))


def pack_updates(flat_updates, chosen, position, is_live, peer_count, capacity):
    picked = flat_updates[chosen]
    picked = jnp.where(is_live[:, None, None], picked, jnp.zeros_like(picked))
    buffer = (
        jnp.zeros((peer_count * capacity,) + picked.shape[1:], picked.dtype)
        .at[position]
        .set(picked)
    )
    return buffer.reshape((peer_count, capacity) + picked.shape[1:])


def assemble(received, labels, targets):
    arrived = received.reshape((-1,) + received.shape[2:])
    flat_labels = labels.reshape(-1)
    select = (flat_labels[None, :] == jnp.arange(targets, dtype=jnp.int32)[:, None]).astype(
        jnp.bfloat16
    )
    return jnp.einsum("tn,nrc->trc", select, arrived, preferred_element_type=jnp.float32)


def pair_products(own_rows, piece_rows):
    blocks = own_rows.shape[1]
    upper_table = np.array([a for a in range(blocks) for b in range(a + 1)], np.int32)
    lower_table = np.array([b for a in range(blocks) for b in range(a + 1)], np.int32)
    left_rows = own_rows[:, upper_table]
    right_rows = piece_rows[:, lower_table]
    return jnp.einsum(
        "fprw,fpcw->fprc", left_rows, right_rows, preferred_element_type=jnp.float32
    ).astype(jnp.bfloat16)


def kernel(
    chips, capacity, split, src_block, owner, target, counts, own, parent, out,
    table, from_x, from_y, product, kept, summed, to_pair, from_pair, to_chip, from_chip,
    to_back, from_back,
    x_send, x_recv, y_send, y_recv, p_send, p_recv, z_send, z_recv, b_send, b_recv,
):
    fronts, blocks, quarter, width = own.shape
    targets = parent.shape[0]
    pairs = blocks * (blocks + 1) // 2
    slots = src_block.shape[1]
    g, c = lax.axis_index("grp"), lax.axis_index("col")
    gy, gx = g // 2, g % 2
    z, core = c // 2, c % 2
    x_peer = gy * 2 + (1 - gx)
    y_peer = (1 - gy) * 2 + gx
    d_peer = 3 - g
    to_x, to_y = {"grp": x_peer, "col": c}, {"grp": y_peer, "col": c}
    to_core = {"grp": g, "col": z * 2 + 1 - core}
    far = [lax.rem(z + hop, chips) for hop in range(1, chips)]
    to_far = [{"grp": g, "col": chip * 2 + core} for chip in far]

    barrier = pltpu.get_barrier_semaphore()
    peers = [to_x, to_y, to_core] + to_far
    for peer in peers:
        pl.semaphore_signal(barrier, inc=1, device_id=peer, device_id_type=MESH)
    pl.semaphore_wait(barrier, len(peers))

    def remote(src, dst, send, recv, device):
        return pltpu.make_async_remote_copy(
            src_ref=src, dst_ref=dst, send_sem=send, recv_sem=recv,
            device_id=device, device_id_type=MESH,
        )

    piece = quarter // split
    x_copy, y_copy = [], []
    for k in range(split):
        at = pl.ds(k * piece, piece)
        x_copy.append(
            remote(own.at[:, :, at], from_x[k], x_send.at[k], x_recv.at[k], to_x)
        )
        y_copy.append(
            remote(own.at[:, :, at], from_y[k], y_send.at[k], y_recv.at[k], to_y)
        )
        x_copy[k].start()
        y_copy[k].start()

    def list_owner(o, carry):
        def look(s, state):
            count, chosen, label = state
            mine = owner[0, s] == o
            named = jnp.where(s < counts[0], target[0, s] + 1, 0)
            hits = [jnp.logical_and(mine, count == k) for k in range(capacity)]
            return (
                count + jnp.where(mine, 1, 0),
                tuple(jnp.where(hits[k], src_block[0, s], chosen[k]) for k in range(capacity)),
                tuple(jnp.where(hits[k], named, label[k]) for k in range(capacity)),
            )

        none = tuple(jnp.int32(0) for _ in range(capacity))
        _, chosen, label = lax.fori_loop(0, slots, look, (jnp.int32(0), none, none))
        for k in range(capacity):
            table[0, o * capacity + k] = chosen[k]
            table[1, o * capacity + k] = label[k]
        return carry

    lax.fori_loop(0, 2 * chips, list_owner, 0)

    def place(n, source, against, pieces):
        high = quarter // pieces
        share = len(source) // pieces
        return [
            (source[i * share:(i + 1) * share], high, against, n * quarter + i * high)
            for i in range(pieces)
        ]

    units = (
        place(0, [own], [own], 1)
        + [
            ([from_x[k], from_y[k]], 2 * piece, [own], quarter + k * 2 * piece)
            for k in range(split)
        ]
        + place(3, from_y, from_x, 2)
    )
    u_own, u_near, u_d = 0, list(range(1, 1 + split)), [1 + split, 2 + split]
    tile = 32

    p_copy, z_copy = [], []
    for u in range(len(units)):
        p_copy.append(remote(to_pair[u], from_pair[u], p_send.at[u], p_recv.at[u], to_core))
        z_copy.append([
            remote(
                to_chip[u].at[h], from_chip[u].at[h],
                z_send.at[u, h], z_recv.at[u, h], to_far[h],
            )
            for h in range(chips - 1)
        ])

    def select(high, parity, store):
        def chip(zz, carry):
            base = (zz * 2 + parity) * capacity
            chosen = [table[0, base + k] for k in range(capacity)]
            label = [table[1, base + k] for k in range(capacity)]
            weight = [
                [jnp.where(label[k] == t + 1, 1.0, 0.0).astype(jnp.float32) for t in range(targets)]
                for k in range(capacity)
            ]

            def rows(i, carry):
                start = pl.multiple_of(i * tile, tile)
                taken = [
                    product[chosen[k], pl.ds(start, tile), :].astype(jnp.float32)
                    for k in range(capacity)
                ]
                for t in range(targets):
                    total = taken[0] * weight[0][t]
                    for k in range(1, capacity):
                        total = total + taken[k] * weight[k][t]
                    store(zz, t, start, total)
                return carry

            return lax.fori_loop(0, high // tile, rows, carry)

        lax.fori_loop(0, chips, chip, 0)

    def make(u):
        source, high, against, _ = units[u]

        def front(f, carry):
            for b in range(blocks):
                left = jnp.concatenate([ref[f, b] for ref in source], axis=0)
                right = jnp.concatenate(
                    [ref[f, a] for a in range(b, blocks) for ref in against], axis=0
                )
                made = lax.dot_general(
                    left, right, (((1,), (1,)), ((), ())),
                    preferred_element_type=jnp.float32,
                ).astype(jnp.bfloat16)
                for a in range(b, blocks):
                    at = f * pairs + a * (a + 1) // 2 + b
                    product[at, :high] = made[:, (a - b) * quarter:(a - b + 1) * quarter]
            return carry

        lax.fori_loop(0, fronts, front, 0)

        def store_pair(zz, t, start, total):
            to_pair[u][zz, t, pl.ds(start, tile), :] = total.astype(jnp.bfloat16)

        def store_kept(zz, t, start, total):
            kept[zz, t, pl.ds(start, tile), :] = total

        select(high, 1 - core, store_pair)
        p_copy[u].start()
        select(high, core, store_kept)

    def pass_on(u):
        _, high, _, row = units[u]
        at = slice(row, row + high)
        p_copy[u].wait_recv()
        for h in range(chips - 1):
            to_chip[u][h] = (
                kept[far[h], :, :high] + from_pair[u][far[h]].astype(jnp.float32)
            ).astype(jnp.bfloat16)
            z_copy[u][h].start()
        summed[:, at] = kept[z, :, :high] + from_pair[u][z].astype(jnp.float32)

    def finish(u):
        _, high, _, row = units[u]
        at = slice(row, row + high)
        for h in range(chips - 1):
            z_copy[u][h].wait_recv()
        total = summed[:, at]
        for h in range(chips - 1):
            total = total + from_chip[u][h].astype(jnp.float32)
        return total

    def settle(u):
        _, high, _, row = units[u]
        summed[:, row:row + high] = finish(u)

    def write(member, total_of):
        at = pl.ds(pl.multiple_of(member * quarter, quarter), quarter)
        for t in range(targets):
            out[t, :, at] = parent[t, :, at] - total_of(t).T

    def near(first):
        parts = [slice(units[u][3] + first, units[u][3] + first + piece) for u in u_near]
        return lambda t: jnp.concatenate([summed[t, part] for part in parts], axis=0)

    make(u_own)
    pass_on(u_own)
    for k in range(split - 1):
        x_copy[k].wait_recv()
        y_copy[k].wait_recv()
        make(u_near[k])
        pass_on(u_near[k])
    settle(u_own)
    write(g, lambda t: summed[t, :quarter])
    x_copy[-1].wait_recv()
    y_copy[-1].wait_recv()
    for u in u_d + u_near[-1:]:
        make(u)
        pass_on(u)
    for k in range(split - 1):
        settle(u_near[k])
    back = []
    for i, u in enumerate(u_d):
        to_back[i][...] = finish(u)
        back.append(remote(to_back[i], from_back[i], b_send.at[i], b_recv.at[i], to_x))
        back[i].start()
    settle(u_near[-1])
    write(x_peer, near(0))
    write(y_peer, near(piece))
    for copy in back:
        copy.wait_recv()
    write(d_peer, lambda t: jnp.concatenate([ref[t] for ref in from_back], axis=0))
    for copy in x_copy + y_copy + p_copy + back:
        copy.wait_send()
    for row in z_copy:
        for copy in row:
            copy.wait_send()


def fused(panels, parent, src_block, dest_owner, target, counts, chips, capacity):
    fronts, blocks, quarter, width = panels.shape
    targets = parent.shape[0]
    pairs = blocks * (blocks + 1) // 2
    split = 4
    units = 3 + split
    piece = pltpu.VMEM((fronts, blocks, quarter // split, width), panels.dtype)
    heights = [quarter] + [2 * quarter // split] * split + [quarter // 2] * 2

    def buffers(count):
        return [pltpu.VMEM((count, targets, high, quarter), jnp.bfloat16) for high in heights]

    last = (targets, quarter, quarter)
    half = pltpu.VMEM((targets, quarter // 2, quarter), jnp.float32)
    dma = pltpu.SemaphoreType.DMA
    scalars = pl.BlockSpec(memory_space=pltpu.SMEM)
    arrays = pl.BlockSpec(memory_space=pltpu.VMEM)
    return pl.pallas_call(
        functools.partial(kernel, chips, capacity, split),
        out_shape=jax.ShapeDtypeStruct(parent.shape, parent.dtype),
        in_specs=[scalars] * 4 + [arrays] * 2,
        out_specs=arrays,
        scratch_shapes=[
            pltpu.SMEM((2, 2 * chips * capacity), jnp.int32),
            [piece] * split, [piece] * split,
            pltpu.VMEM((fronts * pairs, quarter, quarter), jnp.bfloat16),
            pltpu.VMEM((chips,) + last, jnp.float32),
            pltpu.VMEM((targets, 4 * quarter, quarter), jnp.float32),
            buffers(chips), buffers(chips), buffers(chips - 1), buffers(chips - 1),
            [half, half], [half, half],
            dma((split,)), dma((split,)), dma((split,)), dma((split,)),
            dma((units,)), dma((units,)), dma((units, chips - 1)), dma((units, chips - 1)),
            dma((2,)), dma((2,)),
        ],
        compiler_params=pltpu.CompilerParams(
            collective_id=0, has_side_effects=True, vmem_limit_bytes=60 * 1024 * 1024
        ),
    )(src_block, dest_owner.reshape(1, -1), target.reshape(1, -1), counts, panels, parent)


def per_device(panels, parent, src_block, dest_owner, target, counts):
    fronts, blocks, quarter, _ = panels.shape
    pair_count = blocks * (blocks + 1) // 2
    peer_count = lax.axis_size("col")
    slot_count = src_block.shape[1]
    capacity = (slot_count + peer_count - 1) // peer_count + slot_count // (2 * peer_count)
    targets = parent.shape[0]
    if lax.axis_size("grp") == 4 and peer_count % 2 == 0 and targets < capacity:
        return fused(
            panels, parent, src_block, dest_owner, target, counts, peer_count // 2, capacity
        )
    chosen, position, is_live, routed = place_slots(
        src_block, dest_owner, target, counts, peer_count, capacity
    )
    products = pair_products(panels, lax.all_gather(panels, "grp", axis=2, tiled=True))
    flat_updates = products.reshape(fronts * pair_count, quarter, products.shape[3])
    buffer = pack_updates(flat_updates, chosen, position, is_live, peer_count, capacity)
    received, labels = (
        lax.all_to_all(buffer, "col", split_axis=0, concat_axis=0, tiled=True),
        lax.all_to_all(routed, "col", split_axis=0, concat_axis=0, tiled=True),
    )
    return parent - assemble(received, labels, targets)


def solution(mesh):
    placed = (
        P("col", None, "grp", None),
        P("col", "grp", None),
        P("col", None),
        P("col", None),
        P("col"),
        P("col"),
    )
    return jax.shard_map(
        per_device, mesh=mesh, in_specs=placed, out_specs=P("col", "grp", None), check_vma=False
    )
```

profile of v0, /device:TPU:0, one launch (start us, length us, event | category | flops | bytes accessed | tf_op | source)
XLA Modules:
  0.0 82.0 jit_solution(17389685602503184483)
XLA Ops:
  0.7 79.1 %shard_map.64 = f32[4,128,512]{2,1,0:T(8,128)} custom-call(s32[1,40]{1,0:T(1,128)} %src_block.1, s32[1,40]{1,0:T(1,128)} %bitcast.2, s32[1,40]{1,0:T(1,128)} %bitcast.3, s32[1]{0:T(128)S(6)} %copy.8.counts, bf16[4,4,128,512]{3,2,1,0:T(8,128)(2,1)} %own.1, f32[4,128,512]{2,1,0:T(8,128)} %parent.1), custom_call_target="tpu_custom_call" | custom-call | tf_op jit(solution)/shard_map/pallas_call | solution.py:299
  79.7 2.3 %copy.9 = f32[4,128,512]{2,1,0:T(8,128)} copy(f32[4,128,512]{2,1,0:T(8,128)} %shard_map.64) | data formatting | bytes 2097152
where the time goes:
time: 82.1 us; the launch traced here: 82 us
  Pallas kernels  79.1 us (96%)
  local copies, waits for them, and re-layouts  2.26 us (3%)
    pallas_call x1, Pallas kernels, fused(): pl.pallas_call(functools.partial(kernel, chips, capacity, split), out_sha...  79.1 us
    unnamed x1, local copies, waits for them, and re-layouts  2.26 us

commit v1 on v0

v1 whole, which is shorter than its diff:
```python
import functools

import jax
import jax.numpy as jnp
import numpy as np
from jax import lax
from jax.experimental import pallas as pl
from jax.experimental.pallas import tpu as pltpu
from jax.sharding import PartitionSpec as P

MESH = pl.DeviceIdType.MESH


def place_slots(src_block, dest_owner, target, counts, peer_count, capacity):
    slot_count = src_block.shape[1]
    slot_index = jnp.arange(slot_count, dtype=jnp.int32)
    owner_rank = dest_owner[:, 0]
    matches = (owner_rank[:, None] == jnp.arange(peer_count, dtype=jnp.int32)[None, :]).astype(
        jnp.int32
    )
    earlier = jnp.cumsum(matches, axis=0) - matches
    rank_in = jnp.sum(earlier * matches, axis=1)
    position = owner_rank * capacity + rank_in
    is_live = slot_index < counts[0]
    routed = jnp.zeros((peer_count * capacity,), jnp.int32).at[position].set(target)
    return (src_block[0], position, is_live, routed.reshape(peer_count, capacity))


def pack_updates(flat_updates, chosen, position, is_live, peer_count, capacity):
    picked = flat_updates[chosen]
    picked = jnp.where(is_live[:, None, None], picked, jnp.zeros_like(picked))
    buffer = (
        jnp.zeros((peer_count * capacity,) + picked.shape[1:], picked.dtype)
        .at[position]
        .set(picked)
    )
    return buffer.reshape((peer_count, capacity) + picked.shape[1:])


def assemble(received, labels, targets):
    arrived = received.reshape((-1,) + received.shape[2:])
    flat_labels = labels.reshape(-1)
    select = (flat_labels[None, :] == jnp.arange(targets, dtype=jnp.int32)[:, None]).astype(
        jnp.bfloat16
    )
    return jnp.einsum("tn,nrc->trc", select, arrived, preferred_element_type=jnp.float32)


def pair_products(own_rows, piece_rows):
    blocks = own_rows.shape[1]
    upper_table = np.array([a for a in range(blocks) for b in range(a + 1)], np.int32)
    lower_table = np.array([b for a in range(blocks) for b in range(a + 1)], np.int32)
    left_rows = own_rows[:, upper_table]
    right_rows = piece_rows[:, lower_table]
    return jnp.einsum(
        "fprw,fpcw->fprc", left_rows, right_rows, preferred_element_type=jnp.float32
    ).astype(jnp.bfloat16)


def plan(quarter):
    sizes = [quarter // 4] * 3 + [quarter // 8] * 2
    ends = [sum(sizes[: k + 1]) for k in range(len(sizes))]
    middle = ends.index(quarter // 2)
    units = [("own", 0, quarter)]
    for k, size in enumerate(sizes):
        if k == middle:
            units.append(("cross", k, quarter // 2))
        if k > middle:
            units.append(("tie", k, size))
        units.append(("near", k, 2 * size))
    return sizes, ends, middle, units


def kernel(
    chips, capacity, src_block, owner, target, counts, own, parent, out,
    table, from_x, from_y, product, kept, summed, to_pair, from_pair, to_chip, from_chip,
    to_back, from_back,
    x_send, x_recv, y_send, y_recv, p_send, p_recv, z_send, z_recv, b_send, b_recv,
):
    fronts, blocks, quarter, width = own.shape
    targets = parent.shape[0]
    pairs = blocks * (blocks + 1) // 2
    slots = src_block.shape[1]
    half = quarter // 2
    sizes, ends, middle, units = plan(quarter)
    last = len(sizes) - 1
    unit_of = {(kind, k): u for u, (kind, k, _) in enumerate(units)}
    g, c = lax.axis_index("grp"), lax.axis_index("col")
    gy, gx = g // 2, g % 2
    z, core = c // 2, c % 2
    x_peer = gy * 2 + (1 - gx)
    y_peer = (1 - gy) * 2 + gx
    d_peer = 3 - g
    to_x, to_y = {"grp": x_peer, "col": c}, {"grp": y_peer, "col": c}
    to_core = {"grp": g, "col": z * 2 + 1 - core}
    far = [lax.rem(z + hop, chips) for hop in range(1, chips)]
    to_far = [{"grp": g, "col": chip * 2 + core} for chip in far]

    barrier = pltpu.get_barrier_semaphore()
    peers = [to_x, to_y, to_core] + to_far
    for peer in peers:
        pl.semaphore_signal(barrier, inc=1, device_id=peer, device_id_type=MESH)
    pl.semaphore_wait(barrier, len(peers))

    def remote(src, dst, send, recv, device):
        return pltpu.make_async_remote_copy(
            src_ref=src, dst_ref=dst, send_sem=send, recv_sem=recv,
            device_id=device, device_id_type=MESH,
        )

    def x_rows(k):
        return slice(ends[k] - sizes[k], ends[k])

    def y_rows(k):
        return slice(quarter - ends[k], quarter - ends[k] + sizes[k])

    def static(rows):
        return pl.ds(rows.start, rows.stop - rows.start)

    x_copy, y_copy = [], []
    for k in range(len(sizes)):
        at_x, at_y = static(x_rows(k)), static(y_rows(k))
        x_copy.append(
            remote(own.at[:, :, at_x], from_x.at[:, :, at_x], x_send.at[k], x_recv.at[k], to_x)
        )
        y_copy.append(
            remote(own.at[:, :, at_y], from_y.at[:, :, at_y], y_send.at[k], y_recv.at[k], to_y)
        )
        x_copy[k].start()
        y_copy[k].start()

    bits = (fronts * pairs * 8 - 1).bit_length()
    per_word = 31 // bits
    words = -(-capacity // per_word)
    mask = (1 << (bits * per_word)) - 1

    def list_owners(first, count):
        def look(s, state):
            value = src_block[0, s] * 8 + jnp.where(s < counts[0], target[0, s] + 1, 0)
            named = owner[0, s]
            after = []
            for i in range(count):
                mine = named == first + i
                held = state[i * words:(i + 1) * words]
                carry = value
                for word in held:
                    moved = ((word << bits) & mask) | carry
                    carry = word >> (bits * (per_word - 1))
                    after.append(jnp.where(mine, moved, word))
            return tuple(after)

        state = lax.fori_loop(0, slots, look, (jnp.int32(0),) * (words * count))
        for i in range(count):
            for k in range(capacity):
                word = state[i * words + k // per_word]
                item = (word >> (bits * (k % per_word))) & ((1 << bits) - 1)
                table[0, (first + i) * capacity + k] = item >> 3
                table[1, (first + i) * capacity + k] = item & 7

    for first in range(0, 2 * chips, 4):
        list_owners(first, min(4, 2 * chips - first))

    p_copy, z_copy = [], []
    for u in range(len(units)):
        p_copy.append(remote(to_pair[u], from_pair[u], p_send.at[u], p_recv.at[u], to_core))
        z_copy.append([
            remote(
                to_chip[u].at[h], from_chip[u].at[h],
                z_send.at[u, h], z_recv.at[u, h], to_far[h],
            )
            for h in range(chips - 1)
        ])

    def select(high, parity, store):
        tile = min(32, high)

        def chip(zz, carry):
            base = (zz * 2 + parity) * capacity
            chosen = [table[0, base + k] for k in range(capacity)]
            label = [table[1, base + k] for k in range(capacity)]
            weight = [
                [jnp.where(label[k] == t + 1, 1.0, 0.0).astype(jnp.float32) for t in range(targets)]
                for k in range(capacity)
            ]

            def rows(i, carry):
                start = pl.multiple_of(i * tile, tile)
                taken = [
                    product[chosen[k], pl.ds(start, tile), :].astype(jnp.float32)
                    for k in range(capacity)
                ]
                for t in range(targets):
                    total = taken[0] * weight[0][t]
                    for k in range(1, capacity):
                        total = total + taken[k] * weight[k][t]
                    store(zz, t, start, tile, total)
                return carry

            return lax.fori_loop(0, high // tile, rows, carry)

        lax.fori_loop(0, chips, chip, 0)

    def dot(left, right):
        return lax.dot_general(
            left, right, (((1,), (1,)), ((), ())), preferred_element_type=jnp.float32
        ).astype(jnp.bfloat16)

    def stack(f, parts):
        return [jnp.concatenate([ref[f, b, rows] for ref, rows in parts], axis=0) for b in range(blocks)]

    every = slice(0, quarter)

    def against_own(f, parts, high):
        left = stack(f, parts)
        for first in range(0, blocks, 2):
            width_of = min(2, blocks - first)
            right = jnp.concatenate([own[f, first + i] for i in range(width_of)], axis=0)
            made = dot(jnp.concatenate(left[:first + width_of], axis=0), right)
            for i in range(width_of):
                a = first + i
                for b in range(a + 1):
                    product[f * pairs + a * (a + 1) // 2 + b, :high] = made[
                        b * high:(b + 1) * high, i * quarter:(i + 1) * quarter
                    ]

    def grid(f, left, left_rows, right, right_rows):
        return dot(
            jnp.concatenate(stack(f, [(left, left_rows)]), axis=0),
            jnp.concatenate(stack(f, [(right, right_rows)]), axis=0),
        )

    def paired(f, high, lower, upper):
        for a in range(blocks):
            for b in range(a + 1):
                product[f * pairs + a * (a + 1) // 2 + b, :high] = jnp.concatenate(
                    [lower(a, b), upper(a, b)], axis=1
                )

    def make(u):
        kind, k, high = units[u]

        def front(f, carry):
            if kind == "own":
                against_own(f, [(own, every)], high)
            elif kind == "near":
                against_own(f, [(from_x, x_rows(k)), (from_y, y_rows(k))], high)
            elif kind == "cross":
                made = grid(f, from_y, slice(half, quarter), from_x, slice(0, half))

                def piece(p, q):
                    return made[p * high:(p + 1) * high, q * half:(q + 1) * half]

                paired(f, high, lambda a, b: piece(b, a), lambda a, b: piece(a, b))
            else:
                by_y = grid(f, from_y, y_rows(k), from_x, slice(0, half))
                by_x = grid(f, from_x, x_rows(k), from_y, slice(half, quarter))

                def piece(made, p, q):
                    return made[p * high:(p + 1) * high, q * half:(q + 1) * half]

                paired(
                    f, high, lambda a, b: piece(by_y, b, a), lambda a, b: piece(by_x, a, b)
                )
            return carry

        lax.fori_loop(0, fronts, front, 0)

        def store_pair(zz, t, start, tile, total):
            to_pair[u][zz, t, pl.ds(start, tile), :] = total.astype(jnp.bfloat16)

        def store_kept(zz, t, start, tile, total):
            kept[u][zz, t, pl.ds(start, tile), :] = total

        select(high, 1 - core, store_pair)
        p_copy[u].start()
        select(high, core, store_kept)

    def pass_on(u):
        p_copy[u].wait_recv()
        for h in range(chips - 1):
            to_chip[u][h] = (
                kept[u][far[h]] + from_pair[u][far[h]].astype(jnp.float32)
            ).astype(jnp.bfloat16)
            z_copy[u][h].start()
        summed[u][...] = kept[u][z] + from_pair[u][z].astype(jnp.float32)

    def finish(u):
        for h in range(chips - 1):
            z_copy[u][h].wait_recv()
        total = summed[u][...]
        for h in range(chips - 1):
            total = total + from_chip[u][h].astype(jnp.float32)
        return total

    def settle(u):
        summed[u][...] = finish(u)

    corner = [unit_of["cross", middle]] + [unit_of["tie", k] for k in range(middle + 1, last + 1)]
    back = []

    def send_back(i):
        to_back[i][...] = finish(corner[i]).astype(jnp.bfloat16)
        back.append(remote(to_back[i], from_back[i], b_send.at[i], b_recv.at[i], to_x))
        back[-1].start()
        if i == 0:
            at = len(corner)
            back.append(remote(to_back[0], from_back[at], b_send.at[at], b_recv.at[at], to_y))
            back[-1].start()

    def write(member, total_of):
        at = pl.ds(pl.multiple_of(member * quarter, quarter), quarter)
        for t in range(targets):
            out[t, :, at] = parent[t, :, at] - total_of(t)

    def near_x(t):
        return jnp.concatenate(
            [summed[unit_of["near", k]][t, :sizes[k]] for k in range(len(sizes))], axis=0
        ).T

    def near_y(t):
        return jnp.concatenate(
            [summed[unit_of["near", k]][t, sizes[k]:] for k in reversed(range(len(sizes)))], axis=0
        ).T

    def diagonal(t):
        ties = list(range(1, len(corner)))
        turned = jnp.concatenate(
            [from_back[i][t].astype(jnp.float32) for i in reversed(ties)]
            + [from_back[0][t].astype(jnp.float32)],
            axis=0,
        )
        upper = turned.T[:half]
        tied = jnp.concatenate([from_back[i][t].astype(jnp.float32) for i in ties], axis=0)
        crossed = from_back[len(corner)][t].astype(jnp.float32)
        lower = jnp.concatenate([crossed[:, half:], tied[:, half:]], axis=1)
        return jnp.concatenate([upper, lower], axis=0)

    def arrive(k):
        x_copy[k].wait_recv()
        y_copy[k].wait_recv()

    u_own = unit_of["own", 0]
    make(u_own)
    pass_on(u_own)
    for k in range(len(sizes)):
        arrive(k)
        new = [unit_of[kind, k] for kind in ("cross", "tie", "near") if (kind, k) in unit_of]
        for u in new:
            make(u)
        for u in new:
            pass_on(u)
        if k == middle:
            settle(u_own)
            write(g, lambda t: summed[u_own][t].T)
        if k > 0:
            settle(unit_of["near", k - 1])
        if k > middle:
            send_back(k - 1 - middle)
    send_back(len(corner) - 1)
    settle(unit_of["near", last])
    write(x_peer, near_x)
    write(y_peer, near_y)
    for copy in back:
        copy.wait_recv()
    write(d_peer, diagonal)
    for copy in x_copy + y_copy + p_copy + back:
        copy.wait_send()
    for row in z_copy:
        for copy in row:
            copy.wait_send()


def fused(panels, parent, src_block, dest_owner, target, counts, chips, capacity):
    fronts, blocks, quarter, width = panels.shape
    targets = parent.shape[0]
    pairs = blocks * (blocks + 1) // 2
    sizes, _, middle, units = plan(quarter)
    heights = [high for _, _, high in units]
    corner = [high for kind, _, high in units if kind in ("cross", "tie")]

    def buffers(count, kind=jnp.bfloat16):
        return [pltpu.VMEM((count, targets, high, quarter), kind) for high in heights]

    def backs(highs):
        return [pltpu.VMEM((targets, high, quarter), jnp.bfloat16) for high in highs]

    whole = pltpu.VMEM((fronts, blocks, quarter, width), panels.dtype)
    dma = pltpu.SemaphoreType.DMA
    scalars = pl.BlockSpec(memory_space=pltpu.SMEM)
    arrays = pl.BlockSpec(memory_space=pltpu.VMEM)
    return pl.pallas_call(
        functools.partial(kernel, chips, capacity),
        out_shape=jax.ShapeDtypeStruct(parent.shape, parent.dtype),
        in_specs=[scalars] * 4 + [arrays] * 2,
        out_specs=arrays,
        scratch_shapes=[
            pltpu.SMEM((2, 2 * chips * capacity), jnp.int32),
            whole, whole,
            pltpu.VMEM((fronts * pairs, quarter, quarter), jnp.bfloat16),
            buffers(chips, jnp.float32),
            [pltpu.VMEM((targets, high, quarter), jnp.float32) for high in heights],
            buffers(chips), buffers(chips), buffers(chips - 1), buffers(chips - 1),
            backs(corner), backs(corner + corner[:1]),
            dma((len(sizes),)), dma((len(sizes),)), dma((len(sizes),)), dma((len(sizes),)),
            dma((len(units),)), dma((len(units),)),
            dma((len(units), chips - 1)), dma((len(units), chips - 1)),
            dma((len(corner) + 1,)), dma((len(corner) + 1,)),
        ],
        compiler_params=pltpu.CompilerParams(
            collective_id=0, has_side_effects=True, vmem_limit_bytes=60 * 1024 * 1024
        ),
    )(src_block, dest_owner.reshape(1, -1), target.reshape(1, -1), counts, panels, parent)


def per_device(panels, parent, src_block, dest_owner, target, counts):
    fronts, blocks, quarter, _ = panels.shape
    pair_count = blocks * (blocks + 1) // 2
    peer_count = lax.axis_size("col")
    slot_count = src_block.shape[1]
    capacity = (slot_count + peer_count - 1) // peer_count + slot_count // (2 * peer_count)
    targets = parent.shape[0]
    if lax.axis_size("grp") == 4 and peer_count % 2 == 0 and targets < capacity and quarter == 128:
        return fused(
            panels, parent, src_block, dest_owner, target, counts, peer_count // 2, capacity
        )
    chosen, position, is_live, routed = place_slots(
        src_block, dest_owner, target, counts, peer_count, capacity
    )
    products = pair_products(panels, lax.all_gather(panels, "grp", axis=2, tiled=True))
    flat_updates = products.reshape(fronts * pair_count, quarter, products.shape[3])
    buffer = pack_updates(flat_updates, chosen, position, is_live, peer_count, capacity)
    received, labels = (
        lax.all_to_all(buffer, "col", split_axis=0, concat_axis=0, tiled=True),
        lax.all_to_all(routed, "col", split_axis=0, concat_axis=0, tiled=True),
    )
    return parent - assemble(received, labels, targets)


def solution(mesh):
    placed = (
        P("col", None, "grp", None),
        P("col", "grp", None),
        P("col", None),
        P("col", None),
        P("col"),
        P("col"),
    )
    return jax.shard_map(
        per_device, mesh=mesh, in_specs=placed, out_specs=P("col", "grp", None), check_vma=False
    )
```

time: 82.1 us -> 76.2 us (0.928)
  Pallas kernels: 79.1 us -> 73.1 us
    pallas_call x1, Pallas kernels: 79.1 us -> 73.1 us  [fused(): pl.pallas_call(functools.partial(kernel, chips, capacity), out_shape=jax....]
where the time goes in v1:
time: 76.2 us; the launch traced here: 76.1 us
  Pallas kernels  73.1 us (96%)
  local copies, waits for them, and re-layouts  2.26 us (3%)
    pallas_call x1, Pallas kernels, fused(): pl.pallas_call(functools.partial(kernel, chips, capacity), out_shape=jax....  73.1 us
    unnamed x1, local copies, waits for them, and re-layouts  2.26 us

profile of v1, /device:TPU:0, one launch (start us, length us, event | category | flops | bytes accessed | tf_op | source)
XLA Modules:
  0.0 76.1 jit_solution(9540892168661282444)
XLA Ops:
  0.7 73.1 %shard_map.64 = f32[4,128,512]{2,1,0:T(8,128)} custom-call(s32[1,40]{1,0:T(1,128)} %src_block.1, s32[1,40]{1,0:T(1,128)} %bitcast.2, s32[1,40]{1,0:T(1,128)} %bitcast.3, s32[1]{0:T(128)S(6)} %copy.8.counts, bf16[4,4,128,512]{3,2,1,0:T(8,128)(2,1)} %own.1, f32[4,128,512]{2,1,0:T(8,128)} %parent.1), custom_call_target="tpu_custom_call" | custom-call | tf_op jit(solution)/shard_map/pallas_call | solution.py:391
  73.8 2.3 %copy.9 = f32[4,128,512]{2,1,0:T(8,128)} copy(f32[4,128,512]{2,1,0:T(8,128)} %shard_map.64) | data formatting | bytes 2097152

commit v2 on v1

--- a/solution.py
+++ b/solution.py
@@ -58,10 +58,10 @@
 
 
 def plan(quarter):
-    sizes = [quarter // 4] * 3 + [quarter // 8] * 2
+    sizes = [quarter // 4] + [quarter // 8] * 6
     ends = [sum(sizes[: k + 1]) for k in range(len(sizes))]
     middle = ends.index(quarter // 2)
-    units = [("own", 0, quarter)]
+    units = [("own", -1, quarter)]
     for k, size in enumerate(sizes):
         if k == middle:
             units.append(("cross", k, quarter // 2))
@@ -72,12 +72,17 @@
 
 
 def kernel(
-    chips, capacity, src_block, owner, target, counts, own, parent, out,
-    table, from_x, from_y, product, kept, summed, to_pair, from_pair, to_chip, from_chip,
-    to_back, from_back,
-    x_send, x_recv, y_send, y_recv, p_send, p_recv, z_send, z_recv, b_send, b_recv,
+    chips, capacity, relays, src_block, owner, target, counts, panels, parent_in, out,
+    table, own, parent, from_x, from_y, product, kept, summed, to_pair, from_pair,
+    to_chip, from_chip, cargo, to_back, from_back, to_home, from_home,
+    x_send, x_recv, y_send, y_recv, p_send, p_recv, z_send, z_recv, c_recv, b_send, b_recv,
+    h_send, h_recv, l_sem,
 ):
     fronts, blocks, quarter, width = own.shape
+    load_own = pltpu.make_async_copy(panels, own, l_sem.at[0])
+    load_parent = pltpu.make_async_copy(parent_in, parent, l_sem.at[1])
+    load_own.start()
+    load_parent.start()
     targets = parent.shape[0]
     pairs = blocks * (blocks + 1) // 2
     slots = src_block.shape[1]
@@ -95,9 +100,18 @@
     to_core = {"grp": g, "col": z * 2 + 1 - core}
     far = [lax.rem(z + hop, chips) for hop in range(1, chips)]
     to_far = [{"grp": g, "col": chip * 2 + core} for chip in far]
+    edge = jnp.logical_or(z == 0, z == chips - 1)
+    beside = z + 1 - 2 * (z % 2)
+    inner = jnp.where(z < 2, 2, 1)
+    outer = jnp.where(z < 2, 3, 0)
+    to_beside, to_inner, to_outer = (
+        {"grp": g, "col": chip * 2 + core} for chip in (beside, inner, outer)
+    )
+    homes = [z] + far
+    to_homes = [{"grp": x_peer, "col": chip * 2 + core} for chip in homes]
 
     barrier = pltpu.get_barrier_semaphore()
-    peers = [to_x, to_y, to_core] + to_far
+    peers = [to_y, to_core] + to_far + to_homes
     for peer in peers:
         pl.semaphore_signal(barrier, inc=1, device_id=peer, device_id_type=MESH)
     pl.semaphore_wait(barrier, len(peers))
@@ -117,6 +131,7 @@
     def static(rows):
         return pl.ds(rows.start, rows.stop - rows.start)
 
+    load_own.wait()
     x_copy, y_copy = [], []
     for k in range(len(sizes)):
         at_x, at_y = static(x_rows(k)), static(y_rows(k))
@@ -160,16 +175,34 @@
     for first in range(0, 2 * chips, 4):
         list_owners(first, min(4, 2 * chips - first))
 
-    p_copy, z_copy = [], []
+    def blocks_out(u):
+        if relays[u]:
+            to, slots_at = [to_beside, to_inner, to_outer], [0, 1, 1]
+        else:
+            to, slots_at = to_far, [0, 1, 2]
+        return [
+            remote(
+                to_chip[u].at[h], from_chip[u].at[slots_at[h]],
+                z_send.at[u, h], z_recv.at[u, slots_at[h]], to[h],
+            )
+            for h in range(chips - 1)
+        ]
+
+    p_copy, z_copy, c_copy = [], [], []
     for u in range(len(units)):
         p_copy.append(remote(to_pair[u], from_pair[u], p_send.at[u], p_recv.at[u], to_core))
-        z_copy.append([
+        z_copy.append(blocks_out(u))
+        c_copy.append([
             remote(
-                to_chip[u].at[h], from_chip[u].at[h],
-                z_send.at[u, h], z_recv.at[u, h], to_far[h],
+                to_chip[u].at[h], cargo[u].at[h - 1],
+                z_send.at[u, h], c_recv.at[u, h - 1], to_beside,
             )
-            for h in range(chips - 1)
-        ])
+            for h in range(1, chips - 1)
+        ] if relays[u] else None)
+    h_copy = [
+        remote(to_home.at[h], from_home.at[h], h_send.at[h], h_recv.at[h], to_homes[h])
+        for h in range(chips)
+    ]
 
     def select(high, parity, store):
         tile = min(32, high)
@@ -196,7 +229,7 @@
                     store(zz, t, start, tile, total)
                 return carry
 
-            return lax.fori_loop(0, high // tile, rows, carry)
+            return lax.fori_loop(0, high // tile, rows, carry, unroll=True)
 
         lax.fori_loop(0, chips, chip, 0)
 
@@ -263,7 +296,7 @@
                 )
             return carry
 
-        lax.fori_loop(0, fronts, front, 0)
+        lax.fori_loop(0, fronts, front, 0, unroll=True)
 
         def store_pair(zz, t, start, tile, total):
             to_pair[u][zz, t, pl.ds(start, tile), :] = total.astype(jnp.bfloat16)
@@ -275,27 +308,55 @@
         p_copy[u].start()
         select(high, core, store_kept)
 
+    def paired_sum(u, chip):
+        return kept[u][chip] + from_pair[u][chip].astype(jnp.float32)
+
     def pass_on(u):
         p_copy[u].wait_recv()
-        for h in range(chips - 1):
-            to_chip[u][h] = (
-                kept[u][far[h]] + from_pair[u][far[h]].astype(jnp.float32)
-            ).astype(jnp.bfloat16)
-            z_copy[u][h].start()
-        summed[u][...] = kept[u][z] + from_pair[u][z].astype(jnp.float32)
+        if u == u_home:
+            for h in range(chips):
+                to_home[h] = paired_sum(u, homes[h]).astype(jnp.bfloat16)
+                h_copy[h].start()
+            return
+        if not relays[u]:
+            for h in range(chips - 1):
+                to_chip[u][h] = paired_sum(u, far[h]).astype(jnp.bfloat16)
+                z_copy[u][h].start()
+        else:
+            @pl.when(edge)
+            def _():
+                for h, chip in ((2, outer), (1, inner)):
+                    to_chip[u][h] = paired_sum(u, chip).astype(jnp.bfloat16)
+                    c_copy[u][h - 1].start()
+
+            to_chip[u][0] = paired_sum(u, beside).astype(jnp.bfloat16)
+            z_copy[u][0].start()
+        summed[u][...] = paired_sum(u, z)
+
+    def relay(u):
+        @pl.when(jnp.logical_not(edge))
+        def _():
+            for h, chip in ((2, outer), (1, inner)):
+                c_copy[u][h - 1].wait_recv()
+                to_chip[u][h] = (
+                    paired_sum(u, chip) + cargo[u][h - 1].astype(jnp.float32)
+                ).astype(jnp.bfloat16)
+                z_copy[u][h].start()
 
     def finish(u):
-        for h in range(chips - 1):
+        count = 2 if relays[u] else chips - 1
+        for h in range(count):
             z_copy[u][h].wait_recv()
         total = summed[u][...]
-        for h in range(chips - 1):
+        for h in range(count):
             total = total + from_chip[u][h].astype(jnp.float32)
         return total
 
     def settle(u):
         summed[u][...] = finish(u)
 
-    corner = [unit_of["cross", middle]] + [unit_of["tie", k] for k in range(middle + 1, last + 1)]
+    u_own, u_home = unit_of["own", -1], unit_of["tie", last]
+    corner = [unit_of["cross", middle]] + [unit_of["tie", k] for k in range(middle + 1, last)]
     back = []
 
     def send_back(i):
@@ -323,14 +384,14 @@
         ).T
 
     def diagonal(t):
-        ties = list(range(1, len(corner)))
-        turned = jnp.concatenate(
-            [from_back[i][t].astype(jnp.float32) for i in reversed(ties)]
-            + [from_back[0][t].astype(jnp.float32)],
-            axis=0,
-        )
+        ties = [from_back[i][t].astype(jnp.float32) for i in range(1, len(corner))]
+        newest = from_home[0, t].astype(jnp.float32)
+        for h in range(1, chips):
+            newest = newest + from_home[h, t].astype(jnp.float32)
+        ties.append(newest)
+        turned = jnp.concatenate(ties[::-1] + [from_back[0][t].astype(jnp.float32)], axis=0)
         upper = turned.T[:half]
-        tied = jnp.concatenate([from_back[i][t].astype(jnp.float32) for i in ties], axis=0)
+        tied = jnp.concatenate(ties, axis=0)
         crossed = from_back[len(corner)][t].astype(jnp.float32)
         lower = jnp.concatenate([crossed[:, half:], tied[:, half:]], axis=1)
         return jnp.concatenate([upper, lower], axis=0)
@@ -339,12 +400,13 @@
         x_copy[k].wait_recv()
         y_copy[k].wait_recv()
 
-    u_own = unit_of["own", 0]
     make(u_own)
     pass_on(u_own)
+    relay(u_own)
+    load_parent.wait()
     for k in range(len(sizes)):
         arrive(k)
-        new = [unit_of[kind, k] for kind in ("cross", "tie", "near") if (kind, k) in unit_of]
+        new = [unit_of[kind, k] for kind in ("tie", "near", "cross") if (kind, k) in unit_of]
         for u in new:
             make(u)
         for u in new:
@@ -352,22 +414,25 @@
         if k == middle:
             settle(u_own)
             write(g, lambda t: summed[u_own][t].T)
-        if k > 0:
-            settle(unit_of["near", k - 1])
-        if k > middle:
-            send_back(k - 1 - middle)
-    send_back(len(corner) - 1)
-    settle(unit_of["near", last])
+            settle(unit_of["near", 0])
+        for u in new:
+            if relays[u]:
+                relay(u)
+    for i in range(len(corner)):
+        send_back(i)
+    for k in range(1, last + 1):
+        settle(unit_of["near", k])
     write(x_peer, near_x)
     write(y_peer, near_y)
-    for copy in back:
+    for copy in back + h_copy:
         copy.wait_recv()
     write(d_peer, diagonal)
-    for copy in x_copy + y_copy + p_copy + back:
+    for copy in x_copy + y_copy + p_copy + back + h_copy:
         copy.wait_send()
-    for row in z_copy:
-        for copy in row:
-            copy.wait_send()
+    for u in range(len(units)):
+        if u != u_home:
+            for copy in z_copy[u]:
+                copy.wait_send()
 
 
 def fused(panels, parent, src_block, dest_owner, target, counts, chips, capacity):
@@ -376,7 +441,8 @@
     pairs = blocks * (blocks + 1) // 2
     sizes, _, middle, units = plan(quarter)
     heights = [high for _, _, high in units]
-    corner = [high for kind, _, high in units if kind in ("cross", "tie")]
+    corner = [high for kind, _, high in units if kind in ("cross", "tie")][:-1]
+    relays = [k <= middle + 0 for _, k, _ in units]
 
     def buffers(count, kind=jnp.bfloat16):
         return [pltpu.VMEM((count, targets, high, quarter), kind) for high in heights]
@@ -388,23 +454,26 @@
     dma = pltpu.SemaphoreType.DMA
     scalars = pl.BlockSpec(memory_space=pltpu.SMEM)
     arrays = pl.BlockSpec(memory_space=pltpu.VMEM)
+    there = pl.BlockSpec(memory_space=pl.ANY)
+    home = pltpu.VMEM((chips, targets, units[-2][2], quarter), jnp.bfloat16)
     return pl.pallas_call(
-        functools.partial(kernel, chips, capacity),
-        out_shape=jax.ShapeDtypeStruct(parent.shape, parent.dtype),
-        in_specs=[scalars] * 4 + [arrays] * 2,
+        functools.partial(kernel, chips, capacity, relays),
+        out_shape=pltpu.VMEM(parent.shape, parent.dtype),
+        in_specs=[scalars] * 4 + [there] * 2,
         out_specs=arrays,
         scratch_shapes=[
             pltpu.SMEM((2, 2 * chips * capacity), jnp.int32),
-            whole, whole,
+            whole, pltpu.VMEM(parent.shape, parent.dtype), whole, whole,
             pltpu.VMEM((fronts * pairs, quarter, quarter), jnp.bfloat16),
             buffers(chips, jnp.float32),
             [pltpu.VMEM((targets, high, quarter), jnp.float32) for high in heights],
             buffers(chips), buffers(chips), buffers(chips - 1), buffers(chips - 1),
-            backs(corner), backs(corner + corner[:1]),
+            buffers(chips - 2), backs(corner), backs(corner + corner[:1]), home, home,
             dma((len(sizes),)), dma((len(sizes),)), dma((len(sizes),)), dma((len(sizes),)),
             dma((len(units),)), dma((len(units),)),
             dma((len(units), chips - 1)), dma((len(units), chips - 1)),
-            dma((len(corner) + 1,)), dma((len(corner) + 1,)),
+            dma((len(units), chips - 2)), dma((len(corner) + 1,)), dma((len(corner) + 1,)),
+            dma((chips,)), dma((chips,)), dma((2,)),
         ],
         compiler_params=pltpu.CompilerParams(
             collective_id=0, has_side_effects=True, vmem_limit_bytes=60 * 1024 * 1024
@@ -419,7 +488,7 @@
     slot_count = src_block.shape[1]
     capacity = (slot_count + peer_count - 1) // peer_count + slot_count // (2 * peer_count)
     targets = parent.shape[0]
-    if lax.axis_size("grp") == 4 and peer_count % 2 == 0 and targets < capacity and quarter == 128:
+    if lax.axis_size("grp") == 4 and peer_count == 8 and targets < capacity and quarter == 128:
         return fused(
             panels, parent, src_block, dest_owner, target, counts, peer_count // 2, capacity
         )

time: 76.2 us -> 65.3 us (0.86)
  Pallas kernels: 73.1 us -> 63.5 us
  local copies, waits for them, and re-layouts: 2.26 us -> 0.97 us
    pallas_call x1, Pallas kernels: 73.1 us -> 63.5 us  [fused(): pl.pallas_call(functools.partial(kernel, chips, capacity, relays), out_sh...]
    unnamed x1, local copies, waits for them, and re-layouts: 2.26 us -> 0.97 us
where the time goes in v2:
time: 65.3 us; the launch traced here: 65.1 us
  Pallas kernels  63.5 us (97%)
  local copies, waits for them, and re-layouts  0.97 us (1%)
  between operations  0.66 us (1%)
    pallas_call x1, Pallas kernels, fused(): pl.pallas_call(functools.partial(kernel, chips, capacity, relays), out_sh...  63.5 us

profile of v2, /device:TPU:0, one launch (start us, length us, event | category | flops | bytes accessed | tf_op | source)
XLA Modules:
  0.0 65.1 jit_solution(5680339797012877096)
XLA Ops:
  0.7 63.5 %shard_map.64 = f32[4,128,512]{2,1,0:T(8,128)S(1)} custom-call(s32[1,40]{1,0:T(1,128)} %src_block.1, s32[1,40]{1,0:T(1,128)} %bitcast.2, s32[1,40]{1,0:T(1,128)} %bitcast.3, s32[1]{0:T(128)S(6)} %copy.9.counts, bf16[4,4,128,512]{3,2,1,0:T(8,128)(2,1)} %panels.1, f32[4,128,512]{2,1,0:T(8,128)} %parent_in.1), custom_call_target="tpu_custom_call" | custom-call | tf_op jit(solution)/shard_map/pallas_call | solution.py:459
  64.2 1.0 %copy.8 = f32[4,128,512]{2,1,0:T(8,128)} copy(f32[4,128,512]{2,1,0:T(8,128)S(1)} %shard_map.64) | data formatting | bytes 2097152

commit v3 on v2

--- a/solution.py
+++ b/solution.py
@@ -71,24 +71,49 @@
     return sizes, ends, middle, units
 
 
+def layout(units, middle):
+    relayed, direct = [], []
+    for u, (kind, k, _) in enumerate(units):
+        (relayed if k <= middle else direct).append(u)
+    home = direct[-2]
+    direct = [u for u in direct if u != home]
+    first = {}
+    counts = []
+    for group in (relayed, direct):
+        row = 0
+        for u in group:
+            first[u] = row
+            row += units[u][2]
+        counts.append(row)
+    return relayed, direct, home, first, counts
+
+
 def kernel(
-    chips, capacity, relays, src_block, owner, target, counts, panels, parent_in, out,
-    table, own, parent, from_x, from_y, product, kept, summed, to_pair, from_pair,
-    to_chip, from_chip, cargo, to_back, from_back, to_home, from_home,
+    chips, capacity, src_block, owner, target, counts, panels, parent_in, out,
+    table, own, parent, from_x, from_y, product, tie_product, kept, summed, to_pair, from_pair,
+    to_chip, from_relay, from_direct, cargo, to_back, from_back, from_back_y, to_home, from_home,
     x_send, x_recv, y_send, y_recv, p_send, p_recv, z_send, z_recv, c_recv, b_send, b_recv,
-    h_send, h_recv, l_sem,
+    ready, h_send, h_recv, l_sem,
 ):
     fronts, blocks, quarter, width = own.shape
-    load_own = pltpu.make_async_copy(panels, own, l_sem.at[0])
-    load_parent = pltpu.make_async_copy(parent_in, parent, l_sem.at[1])
-    load_own.start()
-    load_parent.start()
+    share = quarter // 4
+    load_own = [
+        pltpu.make_async_copy(
+            panels.at[:, :, pl.ds(i * share, share)], own.at[:, :, pl.ds(i * share, share)],
+            l_sem.at[1 + i],
+        )
+        for i in range(4)
+    ]
+    load_parent = pltpu.make_async_copy(parent_in, parent, l_sem.at[0])
+    for i in (0, 3, 1, 2):
+        load_own[i].start()
     targets = parent.shape[0]
     pairs = blocks * (blocks + 1) // 2
     slots = src_block.shape[1]
     half = quarter // 2
     sizes, ends, middle, units = plan(quarter)
     last = len(sizes) - 1
+    relayed, direct, u_home, first_row, (relay_rows, direct_rows) = layout(units, middle)
     unit_of = {(kind, k): u for u, (kind, k, _) in enumerate(units)}
     g, c = lax.axis_index("grp"), lax.axis_index("col")
     gy, gx = g // 2, g % 2
@@ -107,14 +132,41 @@
     to_beside, to_inner, to_outer = (
         {"grp": g, "col": chip * 2 + core} for chip in (beside, inner, outer)
     )
-    homes = [z] + far
+    homes = far + [z]
     to_homes = [{"grp": x_peer, "col": chip * 2 + core} for chip in homes]
 
     barrier = pltpu.get_barrier_semaphore()
-    peers = [to_y, to_core] + to_far + to_homes
-    for peer in peers:
-        pl.semaphore_signal(barrier, inc=1, device_id=peer, device_id_type=MESH)
-    pl.semaphore_wait(barrier, len(peers))
+
+    def greet(semaphore, peers):
+        for peer in peers:
+            pl.semaphore_signal(semaphore, inc=1, device_id=peer, device_id_type=MESH)
+
+    plane = [{"grp": peer, "col": z * 2} for peer in (x_peer, y_peer)]
+    greet(barrier, plane)
+
+    @pl.when(core == 1)
+    def _():
+        greet(barrier, [to_core])
+
+    @pl.when(core == 0)
+    def _():
+        pl.semaphore_wait(barrier, 5)
+        greet(ready.at[0], [to_core])
+
+    @pl.when(core == 1)
+    def _():
+        pl.semaphore_wait(ready.at[0], 1)
+        greet(barrier, to_far + to_homes[:-1])
+
+    def meet_line():
+        @pl.when(core == 1)
+        def _():
+            pl.semaphore_wait(barrier, 2 * (chips - 1))
+            greet(ready.at[1], [to_core])
+
+        @pl.when(core == 0)
+        def _():
+            pl.semaphore_wait(ready.at[1], 1)
 
     def remote(src, dst, send, recv, device):
         return pltpu.make_async_remote_copy(
@@ -131,18 +183,30 @@
     def static(rows):
         return pl.ds(rows.start, rows.stop - rows.start)
 
-    load_own.wait()
-    x_copy, y_copy = [], []
-    for k in range(len(sizes)):
-        at_x, at_y = static(x_rows(k)), static(y_rows(k))
-        x_copy.append(
-            remote(own.at[:, :, at_x], from_x.at[:, :, at_x], x_send.at[k], x_recv.at[k], to_x)
-        )
-        y_copy.append(
-            remote(own.at[:, :, at_y], from_y.at[:, :, at_y], y_send.at[k], y_recv.at[k], to_y)
-        )
-        x_copy[k].start()
-        y_copy[k].start()
+    def panel_copies(rows_of, into, send, recv, to):
+        copies = []
+        for k in range(len(sizes)):
+            rows = static(rows_of(k))
+            parts = [slice(0, fronts)] if k < last else [slice(0, fronts // 2), slice(fronts // 2, fronts)]
+            for part in parts:
+                at = (static(part), slice(None), rows)
+                copies.append(
+                    remote(own.at[at], into.at[at], send.at[0], recv.at[len(copies)], to)
+                )
+        return copies
+
+    x_copy = panel_copies(x_rows, from_x, x_send, x_recv, to_x)
+    y_copy = panel_copies(y_rows, from_y, y_send, y_recv, to_y)
+    load_own[0].wait()
+    x_copy[0].start()
+    load_own[3].wait()
+    y_copy[0].start()
+    load_own[1].wait()
+    load_own[2].wait()
+    load_parent.start()
+    for i in range(1, len(x_copy)):
+        x_copy[i].start()
+        y_copy[i].start()
 
     bits = (fronts * pairs * 8 - 1).bit_length()
     per_word = 31 // bits
@@ -175,36 +239,50 @@
     for first in range(0, 2 * chips, 4):
         list_owners(first, min(4, 2 * chips - first))
 
+    def rows_in(u):
+        return pl.ds(first_row[u], units[u][2])
+
+    def rows_all(u):
+        if u == u_home:
+            return pl.ds(relay_rows + direct_rows, units[u][2])
+        return pl.ds(first_row[u] + (0 if u in relayed else relay_rows), units[u][2])
+
+    early = relayed[:2]
+    z_group = {u: early.index(u) if u in early else 2 for u in relayed}
+    z_group.update({u: 3 if u != direct[-1] else 4 for u in direct})
+
     def blocks_out(u):
-        if relays[u]:
-            to, slots_at = [to_beside, to_inner, to_outer], [0, 1, 1]
+        if u in relayed:
+            to, slots_at, into = [to_beside, to_inner, to_outer], [0, 1, 1], from_relay
         else:
-            to, slots_at = to_far, [0, 1, 2]
+            to, slots_at, into = to_far, [0, 1, 2], from_direct
         return [
             remote(
-                to_chip[u].at[h], from_chip[u].at[slots_at[h]],
-                z_send.at[u, h], z_recv.at[u, slots_at[h]], to[h],
+                to_chip.at[h, :, rows_all(u)], into.at[slots_at[h], :, rows_in(u)],
+                z_send.at[0], z_recv.at[z_group[u]], to[h],
             )
             for h in range(chips - 1)
         ]
 
-    p_copy, z_copy, c_copy = [], [], []
+    p_copy, z_copy, c_copy = {}, {}, {}
     for u in range(len(units)):
-        p_copy.append(remote(to_pair[u], from_pair[u], p_send.at[u], p_recv.at[u], to_core))
-        z_copy.append(blocks_out(u))
-        c_copy.append([
+        p_copy[u] = remote(to_pair[u], from_pair[u], p_send.at[u], p_recv.at[u], to_core)
+        if u != u_home:
+            z_copy[u] = blocks_out(u)
+    for i, u in enumerate(relayed):
+        c_copy[u] = [
             remote(
-                to_chip[u].at[h], cargo[u].at[h - 1],
-                z_send.at[u, h], c_recv.at[u, h - 1], to_beside,
+                to_chip.at[h, :, rows_all(u)], cargo.at[h - 1, :, rows_in(u)],
+                z_send.at[0], c_recv.at[i, h - 1], to_beside,
             )
             for h in range(1, chips - 1)
-        ] if relays[u] else None)
+        ]
     h_copy = [
-        remote(to_home.at[h], from_home.at[h], h_send.at[h], h_recv.at[h], to_homes[h])
+        remote(to_home.at[h], from_home.at[h], h_send.at[0], h_recv.at[0], to_homes[h])
         for h in range(chips)
     ]
 
-    def select(high, parity, store):
+    def select(made, high, parity, store):
         tile = min(32, high)
 
         def chip(zz, carry):
@@ -219,7 +297,7 @@
             def rows(i, carry):
                 start = pl.multiple_of(i * tile, tile)
                 taken = [
-                    product[chosen[k], pl.ds(start, tile), :].astype(jnp.float32)
+                    made[chosen[k], pl.ds(start, tile), :].astype(jnp.float32)
                     for k in range(capacity)
                 ]
                 for t in range(targets):
@@ -231,7 +309,7 @@
 
             return lax.fori_loop(0, high // tile, rows, carry, unroll=True)
 
-        lax.fori_loop(0, chips, chip, 0)
+        lax.fori_loop(0, chips, chip, 0, unroll=True)
 
     def dot(left, right):
         return lax.dot_general(
@@ -262,14 +340,17 @@
             jnp.concatenate(stack(f, [(right, right_rows)]), axis=0),
         )
 
-    def paired(f, high, lower, upper):
+    def paired(into, f, high, lower, upper):
         for a in range(blocks):
             for b in range(a + 1):
-                product[f * pairs + a * (a + 1) // 2 + b, :high] = jnp.concatenate(
+                into[f * pairs + a * (a + 1) // 2 + b, :high] = jnp.concatenate(
                     [lower(a, b), upper(a, b)], axis=1
                 )
 
-    def make(u):
+    def product_of(u):
+        return tie_product if units[u][0] == "tie" else product
+
+    def multiply(u, some):
         kind, k, high = units[u]
 
         def front(f, carry):
@@ -283,7 +364,7 @@
                 def piece(p, q):
                     return made[p * high:(p + 1) * high, q * half:(q + 1) * half]
 
-                paired(f, high, lambda a, b: piece(b, a), lambda a, b: piece(a, b))
+                paired(product, f, high, lambda a, b: piece(b, a), lambda a, b: piece(a, b))
             else:
                 by_y = grid(f, from_y, y_rows(k), from_x, slice(0, half))
                 by_x = grid(f, from_x, x_rows(k), from_y, slice(half, quarter))
@@ -292,11 +373,18 @@
                     return made[p * high:(p + 1) * high, q * half:(q + 1) * half]
 
                 paired(
-                    f, high, lambda a, b: piece(by_y, b, a), lambda a, b: piece(by_x, a, b)
+                    tie_product, f, high, lambda a, b: piece(by_y, b, a), lambda a, b: piece(by_x, a, b)
                 )
             return carry
 
-        lax.fori_loop(0, fronts, front, 0, unroll=True)
+        if some == slice(0, fronts):
+            lax.fori_loop(0, fronts, front, 0, unroll=True)
+        else:
+            for f in range(some.start, some.stop):
+                front(f, 0)
+
+    def add_up(u):
+        high = units[u][2]
 
         def store_pair(zz, t, start, tile, total):
             to_pair[u][zz, t, pl.ds(start, tile), :] = total.astype(jnp.bfloat16)
@@ -304,9 +392,13 @@
         def store_kept(zz, t, start, tile, total):
             kept[u][zz, t, pl.ds(start, tile), :] = total
 
-        select(high, 1 - core, store_pair)
+        select(product_of(u), high, 1 - core, store_pair)
         p_copy[u].start()
-        select(high, core, store_kept)
+        select(product_of(u), high, core, store_kept)
+
+    def make(u):
+        multiply(u, slice(0, fronts))
+        add_up(u)
 
     def paired_sum(u, chip):
         return kept[u][chip] + from_pair[u][chip].astype(jnp.float32)
@@ -318,18 +410,19 @@
                 to_home[h] = paired_sum(u, homes[h]).astype(jnp.bfloat16)
                 h_copy[h].start()
             return
-        if not relays[u]:
+        at = rows_all(u)
+        if u not in relayed:
             for h in range(chips - 1):
-                to_chip[u][h] = paired_sum(u, far[h]).astype(jnp.bfloat16)
+                to_chip[h, :, at] = paired_sum(u, far[h]).astype(jnp.bfloat16)
                 z_copy[u][h].start()
         else:
             @pl.when(edge)
             def _():
                 for h, chip in ((2, outer), (1, inner)):
-                    to_chip[u][h] = paired_sum(u, chip).astype(jnp.bfloat16)
+                    to_chip[h, :, at] = paired_sum(u, chip).astype(jnp.bfloat16)
                     c_copy[u][h - 1].start()
 
-            to_chip[u][0] = paired_sum(u, beside).astype(jnp.bfloat16)
+            to_chip[0, :, at] = paired_sum(u, beside).astype(jnp.bfloat16)
             z_copy[u][0].start()
         summed[u][...] = paired_sum(u, z)
 
@@ -338,35 +431,43 @@
         def _():
             for h, chip in ((2, outer), (1, inner)):
                 c_copy[u][h - 1].wait_recv()
-                to_chip[u][h] = (
-                    paired_sum(u, chip) + cargo[u][h - 1].astype(jnp.float32)
+                to_chip[h, :, rows_all(u)] = (
+                    paired_sum(u, chip) + cargo[h - 1, :, rows_in(u)].astype(jnp.float32)
                 ).astype(jnp.bfloat16)
                 z_copy[u][h].start()
 
+    def arrived(group):
+        members = [u for u in z_group if z_group[u] == group]
+        into, count = (from_relay, chips - 2) if members[0] in relayed else (from_direct, chips - 1)
+        rows = pl.ds(first_row[members[0]], sum(units[u][2] for u in members))
+        remote(
+            to_chip.at[:count, :, rows], into.at[:, :, rows],
+            z_send.at[0], z_recv.at[group], to_beside,
+        ).wait_recv()
+
     def finish(u):
-        count = 2 if relays[u] else chips - 1
-        for h in range(count):
-            z_copy[u][h].wait_recv()
+        into, count = (from_relay, chips - 2) if u in relayed else (from_direct, chips - 1)
         total = summed[u][...]
         for h in range(count):
-            total = total + from_chip[u][h].astype(jnp.float32)
+            total = total + into[h, :, rows_in(u)].astype(jnp.float32)
         return total
 
     def settle(u):
         summed[u][...] = finish(u)
 
-    u_own, u_home = unit_of["own", -1], unit_of["tie", last]
+    u_own = unit_of["own", -1]
     corner = [unit_of["cross", middle]] + [unit_of["tie", k] for k in range(middle + 1, last)]
-    back = []
-
-    def send_back(i):
-        to_back[i][...] = finish(corner[i]).astype(jnp.bfloat16)
-        back.append(remote(to_back[i], from_back[i], b_send.at[i], b_recv.at[i], to_x))
-        back[-1].start()
-        if i == 0:
-            at = len(corner)
-            back.append(remote(to_back[0], from_back[at], b_send.at[at], b_recv.at[at], to_y))
-            back[-1].start()
+    corner_row = [sum(units[v][2] for v in corner[:i]) for i in range(len(corner) + 1)]
+    back = [
+        remote(to_back, from_back, b_send.at[0], b_recv.at[0], to_x),
+        remote(to_back.at[:, :half], from_back_y, b_send.at[1], b_recv.at[1], to_y),
+    ]
+
+    def send_back():
+        for i, u in enumerate(corner):
+            to_back[:, corner_row[i]:corner_row[i + 1]] = finish(u).astype(jnp.bfloat16)
+        for copy in back:
+            copy.start()
 
     def write(member, total_of):
         at = pl.ds(pl.multiple_of(member * quarter, quarter), quarter)
@@ -384,15 +485,19 @@
         ).T
 
     def diagonal(t):
-        ties = [from_back[i][t].astype(jnp.float32) for i in range(1, len(corner))]
+        ties = [from_back[t, half:].astype(jnp.float32)]
         newest = from_home[0, t].astype(jnp.float32)
         for h in range(1, chips):
             newest = newest + from_home[h, t].astype(jnp.float32)
         ties.append(newest)
-        turned = jnp.concatenate(ties[::-1] + [from_back[0][t].astype(jnp.float32)], axis=0)
+        falling = [newest] + [
+            from_back[t, corner_row[i]:corner_row[i + 1]].astype(jnp.float32)
+            for i in reversed(range(len(corner)))
+        ]
+        turned = jnp.concatenate(falling, axis=0)
         upper = turned.T[:half]
         tied = jnp.concatenate(ties, axis=0)
-        crossed = from_back[len(corner)][t].astype(jnp.float32)
+        crossed = from_back_y[t].astype(jnp.float32)
         lower = jnp.concatenate([crossed[:, half:], tied[:, half:]], axis=1)
         return jnp.concatenate([upper, lower], axis=0)
 
@@ -401,38 +506,55 @@
         y_copy[k].wait_recv()
 
     make(u_own)
+    meet_line()
     pass_on(u_own)
     relay(u_own)
     load_parent.wait()
     for k in range(len(sizes)):
+        new = [unit_of[kind, k] for kind in ("tie", "near", "cross") if (kind, k) in unit_of]
         arrive(k)
-        new = [unit_of[kind, k] for kind in ("tie", "near", "cross") if (kind, k) in unit_of]
-        for u in new:
-            make(u)
+        if k < last:
+            for u in new:
+                make(u)
+        else:
+            for u in new:
+                multiply(u, slice(0, fronts // 2))
+            arrive(k + 1)
+            for u in new:
+                multiply(u, slice(fronts // 2, fronts))
+                add_up(u)
         for u in new:
             pass_on(u)
         if k == middle:
-            settle(u_own)
+            for group, u in enumerate(early):
+                arrived(group)
+                settle(u)
             write(g, lambda t: summed[u_own][t].T)
-            settle(unit_of["near", 0])
         for u in new:
-            if relays[u]:
+            if u in relayed:
                 relay(u)
-    for i in range(len(corner)):
-        send_back(i)
-    for k in range(1, last + 1):
+    arrived(2)
+    arrived(3)
+    send_back()
+    for k in range(1, last):
         settle(unit_of["near", k])
+    arrived(4)
+    settle(unit_of["near", last])
     write(x_peer, near_x)
     write(y_peer, near_y)
-    for copy in back + h_copy:
+    for copy in back:
         copy.wait_recv()
+    whole_home = remote(to_home, from_home, h_send.at[0], h_recv.at[0], to_x)
+    whole_home.wait_recv()
     write(d_peer, diagonal)
-    for copy in x_copy + y_copy + p_copy + back + h_copy:
+    for copy in back + [
+        whole_home,
+        remote(own, from_x, x_send.at[0], x_recv.at[0], to_x),
+        remote(own, from_y, y_send.at[0], y_recv.at[0], to_y),
+        *p_copy.values(),
+        remote(to_chip, to_chip, z_send.at[0], z_recv.at[0], to_beside),
+    ]:
         copy.wait_send()
-    for u in range(len(units)):
-        if u != u_home:
-            for copy in z_copy[u]:
-                copy.wait_send()
 
 
 def fused(panels, parent, src_block, dest_owner, target, counts, chips, capacity):
@@ -441,23 +563,27 @@
     pairs = blocks * (blocks + 1) // 2
     sizes, _, middle, units = plan(quarter)
     heights = [high for _, _, high in units]
-    corner = [high for kind, _, high in units if kind in ("cross", "tie")][:-1]
-    relays = [k <= middle + 0 for _, k, _ in units]
-
-    def buffers(count, kind=jnp.bfloat16):
-        return [pltpu.VMEM((count, targets, high, quarter), kind) for high in heights]
-
-    def backs(highs):
-        return [pltpu.VMEM((targets, high, quarter), jnp.bfloat16) for high in highs]
+    relayed, direct, _, _, (relay_rows, direct_rows) = layout(units, middle)
+    tie = units[-2][2]
+    corner_rows = sum(high for kind, _, high in units if kind in ("cross", "tie")) - tie
+
+    def buffer(count, rows):
+        return pltpu.VMEM((count, targets, rows, quarter), jnp.bfloat16)
+
+    def sums(lead):
+        return [pltpu.VMEM(lead + (targets, high, quarter), jnp.float32) for high in heights]
+
+    def back(rows):
+        return pltpu.VMEM((targets, rows, quarter), jnp.bfloat16)
 
     whole = pltpu.VMEM((fronts, blocks, quarter, width), panels.dtype)
     dma = pltpu.SemaphoreType.DMA
     scalars = pl.BlockSpec(memory_space=pltpu.SMEM)
     arrays = pl.BlockSpec(memory_space=pltpu.VMEM)
     there = pl.BlockSpec(memory_space=pl.ANY)
-    home = pltpu.VMEM((chips, targets, units[-2][2], quarter), jnp.bfloat16)
+    home = buffer(chips, tie)
     return pl.pallas_call(
-        functools.partial(kernel, chips, capacity, relays),
+        functools.partial(kernel, chips, capacity),
         out_shape=pltpu.VMEM(parent.shape, parent.dtype),
         in_specs=[scalars] * 4 + [there] * 2,
         out_specs=arrays,
@@ -465,15 +591,16 @@
             pltpu.SMEM((2, 2 * chips * capacity), jnp.int32),
             whole, pltpu.VMEM(parent.shape, parent.dtype), whole, whole,
             pltpu.VMEM((fronts * pairs, quarter, quarter), jnp.bfloat16),
-            buffers(chips, jnp.float32),
-            [pltpu.VMEM((targets, high, quarter), jnp.float32) for high in heights],
-            buffers(chips), buffers(chips), buffers(chips - 1), buffers(chips - 1),
-            buffers(chips - 2), backs(corner), backs(corner + corner[:1]), home, home,
-            dma((len(sizes),)), dma((len(sizes),)), dma((len(sizes),)), dma((len(sizes),)),
-            dma((len(units),)), dma((len(units),)),
-            dma((len(units), chips - 1)), dma((len(units), chips - 1)),
-            dma((len(units), chips - 2)), dma((len(corner) + 1,)), dma((len(corner) + 1,)),
-            dma((chips,)), dma((chips,)), dma((2,)),
+            pltpu.VMEM((fronts * pairs, tie, quarter), jnp.bfloat16),
+            sums((chips,)), sums(()),
+            [buffer(chips, high) for high in heights], [buffer(chips, high) for high in heights],
+            buffer(chips - 1, relay_rows + direct_rows), buffer(chips - 2, relay_rows),
+            buffer(chips - 1, direct_rows), buffer(chips - 2, relay_rows),
+            back(corner_rows), back(corner_rows), back(quarter // 2), home, home,
+            dma((1,)), dma((len(sizes) + 1,)), dma((1,)), dma((len(sizes) + 1,)),
+            dma((len(units),)), dma((len(units),)), dma((1,)), dma((5,)), dma((len(relayed), chips - 2)),
+            dma((2,)), dma((2,)),
+            pltpu.SemaphoreType.REGULAR((2,)), dma((1,)), dma((1,)), dma((5,)),
         ],
         compiler_params=pltpu.CompilerParams(
             collective_id=0, has_side_effects=True, vmem_limit_bytes=60 * 1024 * 1024

time: 65.3 us -> 63.3 us (0.969)
  Pallas kernels: 63.5 us -> 61.5 us
    pallas_call x1, Pallas kernels: 63.5 us -> 61.5 us  [fused(): pl.pallas_call(functools.partial(kernel, chips, capacity), out_shape=pltp...]
where the time goes in v3:
time: 63.3 us; the launch traced here: 63.2 us
  Pallas kernels  61.5 us (97%)
  local copies, waits for them, and re-layouts  0.97 us (2%)
  between operations  0.66 us (1%)
    pallas_call x1, Pallas kernels, fused(): pl.pallas_call(functools.partial(kernel, chips, capacity), out_shape=pltp...  61.5 us

profile of v3, /device:TPU:0, one launch (start us, length us, event | category | flops | bytes accessed | tf_op | source)
XLA Modules:
  0.0 63.2 jit_solution(17375301666613667405)
XLA Ops:
  0.7 61.5 %shard_map.64 = f32[4,128,512]{2,1,0:T(8,128)S(1)} custom-call(s32[1,40]{1,0:T(1,128)} %src_block.1, s32[1,40]{1,0:T(1,128)} %bitcast.2, s32[1,40]{1,0:T(1,128)} %bitcast.3, s32[1]{0:T(128)S(6)} %copy.9.counts, bf16[4,4,128,512]{3,2,1,0:T(8,128)(2,1)} %panels.1, f32[4,128,512]{2,1,0:T(8,128)} %parent_in.1), custom_call_target="tpu_custom_call" | custom-call | tf_op jit(solution)/shard_map/pallas_call | solution.py:585
  62.2 1.0 %copy.8 = f32[4,128,512]{2,1,0:T(8,128)} copy(f32[4,128,512]{2,1,0:T(8,128)S(1)} %shard_map.64) | data formatting | bytes 2097152

commit v4 on v3

--- a/solution.py
+++ b/solution.py
@@ -89,8 +89,8 @@
 
 
 def kernel(
-    chips, capacity, src_block, owner, target, counts, panels, parent_in, out,
-    table, own, parent, from_x, from_y, product, tie_product, kept, summed, to_pair, from_pair,
+    chips, capacity, src_block_in, owner_in, target_in, counts_in, panels, parent_in, out,
+    src_block, owner, target, counts, table, own, parent, from_x, from_y, product, tie_product, kept, summed, to_pair, from_pair,
     to_chip, from_relay, from_direct, cargo, to_back, from_back, from_back_y, to_home, from_home,
     x_send, x_recv, y_send, y_recv, p_send, p_recv, z_send, z_recv, c_recv, b_send, b_recv,
     ready, h_send, h_recv, l_sem,
@@ -107,6 +107,14 @@
     load_parent = pltpu.make_async_copy(parent_in, parent, l_sem.at[0])
     for i in (0, 3, 1, 2):
         load_own[i].start()
+    load_slots = [
+        pltpu.make_async_copy(given, kept_at, l_sem.at[5 + i])
+        for i, (given, kept_at) in enumerate((
+            (src_block_in, src_block), (owner_in, owner), (target_in, target), (counts_in, counts)
+        ))
+    ]
+    for copy in load_slots:
+        copy.start()
     targets = parent.shape[0]
     pairs = blocks * (blocks + 1) // 2
     slots = src_block.shape[1]
@@ -156,7 +164,6 @@
     @pl.when(core == 1)
     def _():
         pl.semaphore_wait(ready.at[0], 1)
-        greet(barrier, to_far + to_homes[:-1])
 
     def meet_line():
         @pl.when(core == 1)
@@ -187,7 +194,7 @@
         copies = []
         for k in range(len(sizes)):
             rows = static(rows_of(k))
-            parts = [slice(0, fronts)] if k < last else [slice(0, fronts // 2), slice(fronts // 2, fronts)]
+            parts = [slice(0, fronts)] if k < last else [slice(f, f + 1) for f in range(fronts)]
             for part in parts:
                 at = (static(part), slice(None), rows)
                 copies.append(
@@ -208,6 +215,10 @@
         x_copy[i].start()
         y_copy[i].start()
 
+    @pl.when(core == 1)
+    def _():
+        greet(barrier, to_far + to_homes[:-1])
+
     bits = (fronts * pairs * 8 - 1).bit_length()
     per_word = 31 // bits
     words = -(-capacity // per_word)
@@ -215,7 +226,7 @@
 
     def list_owners(first, count):
         def look(s, state):
-            value = src_block[0, s] * 8 + jnp.where(s < counts[0], target[0, s] + 1, 0)
+            value = src_block[0, s] * 8 + jnp.where(s < counts[0, 0], target[0, s] + 1, 0)
             named = owner[0, s]
             after = []
             for i in range(count):
@@ -236,6 +247,8 @@
                 table[0, (first + i) * capacity + k] = item >> 3
                 table[1, (first + i) * capacity + k] = item & 7
 
+    for copy in load_slots:
+        copy.wait()
     for first in range(0, 2 * chips, 4):
         list_owners(first, min(4, 2 * chips - first))
 
@@ -249,7 +262,7 @@
 
     early = relayed[:2]
     z_group = {u: early.index(u) if u in early else 2 for u in relayed}
-    z_group.update({u: 3 if u != direct[-1] else 4 for u in direct})
+    z_group.update({u: 3 + max(0, units[u][1] - last + 2) for u in direct})
 
     def blocks_out(u):
         if u in relayed:
@@ -458,15 +471,17 @@
     u_own = unit_of["own", -1]
     corner = [unit_of["cross", middle]] + [unit_of["tie", k] for k in range(middle + 1, last)]
     corner_row = [sum(units[v][2] for v in corner[:i]) for i in range(len(corner) + 1)]
+    split = corner_row[-2]
     back = [
-        remote(to_back, from_back, b_send.at[0], b_recv.at[0], to_x),
-        remote(to_back.at[:, :half], from_back_y, b_send.at[1], b_recv.at[1], to_y),
+        remote(to_back.at[:, :half], from_back_y, b_send.at[0], b_recv.at[0], to_y),
+        remote(to_back.at[:, :split], from_back.at[:, :split], b_send.at[1], b_recv.at[1], to_x),
+        remote(to_back.at[:, split:], from_back.at[:, split:], b_send.at[2], b_recv.at[2], to_x),
     ]
 
-    def send_back():
-        for i, u in enumerate(corner):
-            to_back[:, corner_row[i]:corner_row[i + 1]] = finish(u).astype(jnp.bfloat16)
-        for copy in back:
+    def send_back(which, copies):
+        for i in which:
+            to_back[:, corner_row[i]:corner_row[i + 1]] = finish(corner[i]).astype(jnp.bfloat16)
+        for copy in copies:
             copy.start()
 
     def write(member, total_of):
@@ -517,12 +532,13 @@
             for u in new:
                 make(u)
         else:
-            for u in new:
-                multiply(u, slice(0, fronts // 2))
-            arrive(k + 1)
-            for u in new:
-                multiply(u, slice(fronts // 2, fronts))
-                add_up(u)
+            for f in range(fronts):
+                if f:
+                    arrive(k + f)
+                for u in new:
+                    multiply(u, slice(f, f + 1))
+                    if f == fronts - 1:
+                        add_up(u)
         for u in new:
             pass_on(u)
         if k == middle:
@@ -535,10 +551,13 @@
                 relay(u)
     arrived(2)
     arrived(3)
-    send_back()
-    for k in range(1, last):
+    send_back(range(len(corner) - 1), back[:2])
+    for k in range(1, last - 1):
         settle(unit_of["near", k])
     arrived(4)
+    send_back([len(corner) - 1], back[2:])
+    settle(unit_of["near", last - 1])
+    arrived(5)
     settle(unit_of["near", last])
     write(x_peer, near_x)
     write(y_peer, near_y)
@@ -578,34 +597,35 @@
 
     whole = pltpu.VMEM((fronts, blocks, quarter, width), panels.dtype)
     dma = pltpu.SemaphoreType.DMA
-    scalars = pl.BlockSpec(memory_space=pltpu.SMEM)
+    slots = pltpu.SMEM(src_block.shape, jnp.int32)
     arrays = pl.BlockSpec(memory_space=pltpu.VMEM)
     there = pl.BlockSpec(memory_space=pl.ANY)
     home = buffer(chips, tie)
     return pl.pallas_call(
         functools.partial(kernel, chips, capacity),
         out_shape=pltpu.VMEM(parent.shape, parent.dtype),
-        in_specs=[scalars] * 4 + [there] * 2,
+        in_specs=[there] * 6,
         out_specs=arrays,
         scratch_shapes=[
+            slots, slots, slots, pltpu.SMEM((1, 1), jnp.int32),
             pltpu.SMEM((2, 2 * chips * capacity), jnp.int32),
             whole, pltpu.VMEM(parent.shape, parent.dtype), whole, whole,
             pltpu.VMEM((fronts * pairs, quarter, quarter), jnp.bfloat16),
-            pltpu.VMEM((fronts * pairs, tie, quarter), jnp.bfloat16),
+            pltpu.VMEM((fronts * pairs, quarter // 4, quarter), jnp.bfloat16),
             sums((chips,)), sums(()),
             [buffer(chips, high) for high in heights], [buffer(chips, high) for high in heights],
             buffer(chips - 1, relay_rows + direct_rows), buffer(chips - 2, relay_rows),
             buffer(chips - 1, direct_rows), buffer(chips - 2, relay_rows),
             back(corner_rows), back(corner_rows), back(quarter // 2), home, home,
-            dma((1,)), dma((len(sizes) + 1,)), dma((1,)), dma((len(sizes) + 1,)),
-            dma((len(units),)), dma((len(units),)), dma((1,)), dma((5,)), dma((len(relayed), chips - 2)),
-            dma((2,)), dma((2,)),
-            pltpu.SemaphoreType.REGULAR((2,)), dma((1,)), dma((1,)), dma((5,)),
+            dma((1,)), dma((len(sizes) + fronts,)), dma((1,)), dma((len(sizes) + fronts,)),
+            dma((len(units),)), dma((len(units),)), dma((1,)), dma((6,)), dma((len(relayed), chips - 2)),
+            dma((3,)), dma((3,)),
+            pltpu.SemaphoreType.REGULAR((2,)), dma((1,)), dma((1,)), dma((9,)),
         ],
         compiler_params=pltpu.CompilerParams(
             collective_id=0, has_side_effects=True, vmem_limit_bytes=60 * 1024 * 1024
         ),
-    )(src_block, dest_owner.reshape(1, -1), target.reshape(1, -1), counts, panels, parent)
+    )(src_block, dest_owner.reshape(1, -1), target.reshape(1, -1), counts.reshape(1, 1), panels, parent)
 
 
 def per_device(panels, parent, src_block, dest_owner, target, counts):

time: 63.3 us -> 62.6 us (0.989)
    pallas_call x1, Pallas kernels: 61.5 us -> 60.9 us  [fused(): pl.pallas_call(functools.partial(kernel, chips, capacity), out_shape=pltp...]
where the time goes in v4:
time: 62.6 us; the launch traced here: 62.5 us
  Pallas kernels  60.9 us (97%)
  local copies, waits for them, and re-layouts  0.97 us (2%)
  between operations  0.66 us (1%)
    pallas_call x1, Pallas kernels, fused(): pl.pallas_call(functools.partial(kernel, chips, capacity), out_shape=pltp...  60.9 us

profile of v4, /device:TPU:0, one launch (start us, length us, event | category | flops | bytes accessed | tf_op | source)
XLA Modules:
  0.0 62.5 jit_solution(15762310619907805666)
XLA Ops:
  0.7 60.9 %shard_map.64 = f32[4,128,512]{2,1,0:T(8,128)S(1)} custom-call(s32[1,40]{1,0:T(1,128)} %src_block_in.1, s32[1,40]{1,0:T(1,128)} %bitcast.4, s32[1,40]{1,0:T(1,128)} %bitcast.5, s32[1,1]{1,0:T(1,128)} %bitcast.3.counts_in, bf16[4,4,128,512]{3,2,1,0:T(8,128)(2,1)} %panels.1, f32[4,128,512]{2,1,0:T(8,128)} %parent_in.1), custom_call_target="tpu_custom_call" | custom-call | tf_op jit(solution)/shard_map/pallas_call | solution.py:604
  61.5 1.0 %copy.8 = f32[4,128,512]{2,1,0:T(8,128)} copy(f32[4,128,512]{2,1,0:T(8,128)S(1)} %shard_map.64) | data formatting | bytes 2097152

commit v5 on v4

--- a/solution.py
+++ b/solution.py
@@ -74,7 +74,7 @@
 def layout(units, middle):
     relayed, direct = [], []
     for u, (kind, k, _) in enumerate(units):
-        (relayed if k <= middle else direct).append(u)
+        (relayed if k <= middle - 1 else direct).append(u)
     home = direct[-2]
     direct = [u for u in direct if u != home]
     first = {}
@@ -405,13 +405,19 @@
         def store_kept(zz, t, start, tile, total):
             kept[u][zz, t, pl.ds(start, tile), :] = total
 
-        select(product_of(u), high, 1 - core, store_pair)
-        p_copy[u].start()
-        select(product_of(u), high, core, store_kept)
+        def give():
+            select(product_of(u), high, 1 - core, store_pair)
+            p_copy[u].start()
+
+        def keep():
+            select(product_of(u), high, core, store_kept)
+
+        return give, keep
 
     def make(u):
         multiply(u, slice(0, fronts))
-        add_up(u)
+        for part in add_up(u):
+            part()
 
     def paired_sum(u, chip):
         return kept[u][chip] + from_pair[u][chip].astype(jnp.float32)
@@ -538,7 +544,9 @@
                 for u in new:
                     multiply(u, slice(f, f + 1))
                     if f == fronts - 1:
-                        add_up(u)
+                        add_up(u)[0]()
+            for u in new:
+                add_up(u)[1]()
         for u in new:
             pass_on(u)
         if k == middle:

time: 62.6 us -> 62.7 us (level)
  no operation moved by 1% of the time
where the time goes in v5:
time: 62.7 us; the launch traced here: 62.5 us
  Pallas kernels  60.9 us (97%)
  local copies, waits for them, and re-layouts  0.97 us (2%)
  between operations  0.66 us (1%)
    pallas_call x1, Pallas kernels, fused(): pl.pallas_call(functools.partial(kernel, chips, capacity), out_shape=pltp...  60.9 us

profile of v5, /device:TPU:0, one launch (start us, length us, event | category | flops | bytes accessed | tf_op | source)
XLA Modules:
  0.0 62.5 jit_solution(15671706220575803056)
XLA Ops:
  0.7 60.9 %shard_map.64 = f32[4,128,512]{2,1,0:T(8,128)S(1)} custom-call(s32[1,40]{1,0:T(1,128)} %src_block_in.1, s32[1,40]{1,0:T(1,128)} %bitcast.4, s32[1,40]{1,0:T(1,128)} %bitcast.5, s32[1,1]{1,0:T(1,128)} %bitcast.3.counts_in, bf16[4,4,128,512]{3,2,1,0:T(8,128)(2,1)} %panels.1, f32[4,128,512]{2,1,0:T(8,128)} %parent_in.1), custom_call_target="tpu_custom_call" | custom-call | tf_op jit(solution)/shard_map/pallas_call | solution.py:612
  61.5 1.0 %copy.8 = f32[4,128,512]{2,1,0:T(8,128)} copy(f32[4,128,512]{2,1,0:T(8,128)S(1)} %shard_map.64) | data formatting | bytes 2097152
